TPU v7x, 256 devices: a whole 4x4x8 slice. The times are simulated.
256 devices in a mesh: batch: 16 (over y, x), field: 2 (over core), dim: 8 (over z).
Axes of the slice: x: 4, y: 4, z: 8, core: 2. Of those that a mesh axis runs over, the one named last changes fastest.
Arguments:
- features: bfloat16 [26, 128, 16384], P('field', 'dim', 'batch'), may hold values from -6 to 6
- cross_weight: bfloat16 [2, 26, 128, 26, 128], P(None, 'field', 'dim'), may hold values from -0.109375 to 0.109375
- cross_bias: float32 [2, 26, 128], P(None, 'field', 'dim'), may hold values from -3 to 3
- tower_weight: bfloat16 [1024, 26, 128], P(('field', 'dim')), may hold values from -0.109375 to 0.109375
- tower_bias: float32 [1024], P(('field', 'dim')), may hold values from -3 to 3
- query_weight: bfloat16 [1024, 128], P(('field', 'dim')), may hold values from -0.1875 to 0.1875
- user_vec: bfloat16 [16384, 128], P('batch'), may hold values from -6 to 6
- candidates: bfloat16 [4096, 128], P('batch'), may hold values from -6 to 6
- positive: int32 [16384], P('batch'), may hold values from 0 to 4095
Outputs:
- crossed: bfloat16 [26, 128, 16384], P('field', 'dim', 'batch')
- losses: float32 [16384], P('batch')
All inputs are finite; a program needn't handle non-finite values.
Results may differ from a plain program's by a relative error of at most 0.0049.
Values may be sent and summed in bfloat16 or wider, within the bound.
A program may use at most 64 MiB of HBM per device.

v0:
```python
import math
import jax
import jax.numpy as jnp
from jax import lax
from jax.sharding import Mesh
from jax.sharding import PartitionSpec as P

CROSS = 2
BATCH = ("batch_0", "batch_1")


def whole_of(x, axes, dim):
    if not axes:
        return x
    nearer = lax.all_gather(x, axes[-1], axis=dim, tiled=True)
    return whole_of(nearer, axes[:-1], dim)


def cut_along(x, dim, length):
    shape = x.shape
    pieces = x.reshape(*shape[:dim], length, shape[dim] // length, *shape[dim + 1 :])
    return jnp.moveaxis(pieces, dim, 0)


def summed_on_arrival(x, axis, dim):
    length = lax.axis_size(axis)
    pieces = lax.all_to_all(cut_along(x, dim, length), axis, 0, 0, tiled=True)
    return jnp.sum(pieces.astype(jnp.float32), axis=0)


def laid_out(pieces, dim):
    shape = list(pieces.shape[1:])
    shape[dim] *= pieces.shape[0]
    return jnp.moveaxis(pieces, 0, dim).reshape(shape)


def sent_to_all(x, axis):
    copies = jnp.broadcast_to(x, (lax.axis_size(axis), *x.shape))
    return lax.all_to_all(copies, axis, split_axis=0, concat_axis=0, tiled=True)


def gather_directly(x, axis, dim):
    return laid_out(sent_to_all(x, axis), dim)


def by_device(weights, field_count, dim_count):
    out_count, fields_all, entries_all = weights.shape
    shaped = weights.reshape(
        out_count, field_count, fields_all // field_count, dim_count, entries_all // dim_count
    )
    shaped = shaped.transpose(1, 3, 0, 2, 4)
    return shaped.reshape(
        field_count * dim_count, out_count, fields_all // field_count * (entries_all // dim_count)
    )


def row_adder(blocks, shards):
    return jnp.einsum("kib,koi->ob", shards, blocks, preferred_element_type=jnp.float32)


def cross_flat(current, blocks):
    field_local, entry_local, row_count = current.shape
    flattened = current.reshape(1, field_local * entry_local, row_count)
    return row_adder(blocks, lax.all_gather(flattened, ("field", "dim"), axis=0, tiled=True))


def next_layer(anchor, current, product, bias_vec):
    field_local, entry_local, row_count = current.shape
    gated = (product + bias_vec.reshape(field_local * entry_local, 1)).reshape(
        field_local, entry_local, row_count
    )
    return (anchor * gated + current.astype(jnp.float32)).astype(jnp.bfloat16)


def candidate_loss(query_vec, targets, candidates):
    score_scale = 1.0 / math.sqrt(query_vec.shape[1])
    row_count = query_vec.shape[0]
    running_max = jnp.full((row_count,), -1e30, jnp.float32)
    logits = (
        jnp.einsum(
            "be,ce->bc",
            query_vec,
            whole_of(candidates, BATCH, 0),
            preferred_element_type=jnp.float32,
        )
        * score_scale
    )
    labels = lax.broadcasted_iota(jnp.int32, logits.shape, 1)
    picked = jnp.sum(jnp.where(labels == targets[:, None], logits, 0.0), axis=1)
    new_max = jnp.maximum(running_max, jnp.max(logits, axis=1))
    running_sum = jnp.sum(jnp.exp(logits - new_max[:, None]), axis=1)
    best_score, exp_total, picked = (new_max, running_sum, picked)
    return best_score + jnp.log(exp_total) - picked


def body(
    features,
    cross_weight,
    cross_bias,
    tower_weight,
    tower_bias,
    query_weight,
    user_vec,
    candidates,
    positive,
):
    field_count = lax.axis_size("field")
    dim_count = lax.axis_size("dim")
    field_local, entry_local, row_count = features.shape
    column_count = field_local * entry_local
    anchor = features.astype(jnp.float32)
    current = features
    stacked = cross_weight.reshape(
        CROSS, column_count, cross_weight.shape[3], cross_weight.shape[4]
    )
    for level_idx in range(CROSS):
        blocks = by_device(stacked[level_idx], field_count, dim_count)
        product = cross_flat(current, blocks)
        current = next_layer(anchor, current, product, cross_bias[level_idx])
    tower_blocks = by_device(tower_weight, field_count, dim_count)
    flattened = current.reshape(1, column_count, row_count)
    tower_pre = row_adder(
        tower_blocks, lax.all_gather(flattened, ("field", "dim"), axis=0, tiled=True)
    )
    hidden = jax.nn.relu(tower_pre + tower_bias[:, None]).astype(jnp.bfloat16)
    partial_value = lax.dot_general(
        hidden, query_weight, (((0,), (0,)), ((), ())), preferred_element_type=jnp.float32
    )
    share_rows = row_count // (field_count * dim_count)
    member = lax.axis_index(("field", "dim"))
    query_part = summed_on_arrival(partial_value.astype(jnp.bfloat16), ("field", "dim"), 0)
    user_rows = lax.dynamic_slice_in_dim(user_vec, member * share_rows, share_rows, 0)
    targets = lax.dynamic_slice_in_dim(positive, member * share_rows, share_rows, 0)
    query_vec = (query_part + user_rows.astype(jnp.float32)).astype(jnp.bfloat16)
    part_loss = candidate_loss(query_vec, targets, candidates)
    losses = gather_directly(part_loss, ("field", "dim"), 0)
    return (current, losses)


def solution(mesh):
    torus = Mesh(
        mesh.devices.reshape(4, 4, mesh.shape["field"], mesh.shape["dim"]),
        ("batch_0", "batch_1", "field", "dim"),
    )
    in_specs = (
        P("field", "dim", BATCH),
        P(None, "field", "dim", None, None),
        P(None, "field", "dim"),
        P(("field", "dim"), None, None),
        P(("field", "dim")),
        P(("field", "dim"), None),
        P(BATCH, None),
        P(BATCH, None),
        P(BATCH),
    )
    out_specs = (P("field", "dim", BATCH), P(BATCH))
    return jax.shard_map(body, mesh=torus, in_specs=in_specs, out_specs=out_specs, check_vma=False)
```

profile of v0, /device:TPU:1, one launch (start us, length us, event | category | flops | bytes accessed | tf_op | source)
XLA Modules:
  0.0 219.8 jit_solution(14988092904554589448)
XLA Ops:
  7.2 0.0 copy-start
  7.2 0.0 all-gather.5.cloned.1.call-start
  7.2 0.7 all-gather.5.cloned.1.call-update
  7.9 0.0 all-gather.7.cloned.1.call-start
  8.0 2.2 %fusion.13 = (bf16[1,13,16,26,128]{4,2,3,1,0:T(8,128)(2,1)S(1)}, bf16[1,13,16,26,128]{4,2,3,1,0:T(8,128)(2,1)S(1)}) fusion(bf16[2,13,16,26,128]{4,2,3,1,0:T(8,128)(2,1)} %param.10), kind=kLoop, calls=%fused_computation.29 | loop fusion | bytes 5537792 | tf_op jit(solution)/shard_map/slice | solution.py:117
  10.2 0.2 copy.19
  10.4 8.7 %reshape_squeeze.8 = bf16[208,2,13,8,16]{4,3,0,2,1:T(8,128)(2,1)} reshape(bf16[1,13,16,26,128]{4,2,1,3,0:T(8,128)(2,1)S(1)} %copy.19) | data formatting | bytes 2768896 | tf_op jit(solution)/shard_map/reshape;squeeze | solution.py:48
  19.1 10.9 %copy.20 = bf16[2,8,208,13,16]{2,4,3,1,0:T(8,128)(2,1)S(1)} copy(bf16[2,8,208,13,16]{4,1,2,3,0:T(8,128)(2,1)} %bitcast.50) | data formatting | bytes 2768896 | tf_op jit(solution)/shard_map/transpose | solution.py:51
  30.1 0.0 copy-done.5
  30.1 0.1 add.51
  30.2 32.3 %all-gather.5.cloned.1.call-done = bf16[16,208,1024]{2,1,0:T(8,128)(2,1)} async-done(((bf16[1,208,1024]{2,1,0:T(8,128)(2,1)}), bf16[16,208,1024]{2,1,0:T(8,128)(2,1)}) %all-gather.5.cloned.1.call-update) | async-done | bytes 6815760 | tf_op jit(solution)/shard_map/all_gather | solution.py:64
  62.5 4.6 %fusion = f32[208,1024]{1,0:T(8,128)S(1)} fusion(bf16[16,208,208]{1,2,0:T(8,128)(2,1)S(1)} %bitcast.52, bf16[16,208,1024]{2,1,0:T(8,128)(2,1)} %all-gather.5.cloned.1.call-done, f32[208]{0:T(256)S(1)} %add.51), kind=kOutput, calls=%fused_computation.4 | convolution fusion | flops 1417887744 | bytes 9052992 | tf_op jit(solution)/shard_map/kib,koi->ob/dot_general | solution.py:58
  67.1 0.0 copy-done.1
  67.1 0.9 fusion.7
  68.0 0.0 all-gather.7.cloned.1.call-update
  68.0 0.0 all-gather.9.cloned.1.call-start
  68.1 0.2 copy.22
  68.3 8.7 %reshape_squeeze.9 = bf16[208,2,13,8,16]{4,3,0,2,1:T(8,128)(2,1)} reshape(bf16[1,13,16,26,128]{4,2,1,3,0:T(8,128)(2,1)S(1)} %copy.22) | data formatting | bytes 2768896 | tf_op jit(solution)/shard_map/reshape;squeeze | solution.py:48
  77.0 11.2 %copy.23 = bf16[2,8,208,13,16]{2,4,3,1,0:T(8,128)(2,1)S(1)} copy(bf16[2,8,208,13,16]{4,1,2,3,0:T(8,128)(2,1)} %bitcast.51) | data formatting | bytes 2768896 | tf_op jit(solution)/shard_map/transpose | solution.py:51
  88.2 0.1 add.55
  88.2 26.9 %all-gather.7.cloned.1.call-done = bf16[16,208,1024]{2,1,0:T(8,128)(2,1)} async-done(((bf16[1,208,1024]{2,1,0:T(8,128)(2,1)}), bf16[16,208,1024]{2,1,0:T(8,128)(2,1)}) %all-gather.7.cloned.1.call-update) | async-done | bytes 6815760 | tf_op jit(solution)/shard_map/all_gather | solution.py:64
  115.2 4.6 %fusion.1 = f32[1024,208]{0,1:T(8,128)S(1)} fusion(bf16[16,208,1024]{2,1,0:T(8,128)(2,1)} %all-gather.7.cloned.1.call-done, bf16[16,208,208]{1,2,0:T(8,128)(2,1)S(1)} %bitcast.58, f32[208]{0:T(256)S(1)} %add.55), kind=kOutput, calls=%fused_computation.5 | convolution fusion | flops 1417887744 | bytes 9052992 | tf_op jit(solution)/shard_map/kib,koi->ob/dot_general | solution.py:58
  119.8 0.0 copy-start.3
  119.8 0.0 copy-done.2
  119.8 0.0 copy-start.6
  119.9 1.0 fusion.6
  120.8 0.0 all-gather.9.cloned.1.call-update
  120.8 0.0 all-gather.11.cloned.1.call-start
  120.9 0.0 copy-done.4
  120.9 10.4 %all_gather.18 = bf16[1024,128]{1,0:T(8,128)(2,1)} all-gather(bf16[256,128]{1,0:T(8,128)(2,1)S(1)} %copy-done.4), channel_id=1, replica_groups=mesh['batch_0'=4,'batch_1'=4,'field'=2,'dim'=8] {'batch_1'}, dimensions={0}, use_global_device_ids=true | all-gather | bytes 327680 | tf_op jit(solution)/shard_map/all_gather | solution.py:15
  131.3 0.0 all-gather.11.cloned.1.call-update
  131.4 0.0 copy-done.3
  131.4 0.4 copy.25
  131.8 0.1 copy.26
  132.0 36.0 %all-gather.9.cloned.1.call-done = bf16[16,208,1024]{2,1,0:T(8,128)(2,1)} async-done(((bf16[1,208,1024]{2,1,0:T(8,128)(2,1)}), bf16[16,208,1024]{2,1,0:T(8,128)(2,1)}) %all-gather.9.cloned.1.call-update) | async-done | bytes 6815760 | tf_op jit(solution)/shard_map/all_gather | solution.py:123
  168.0 0.0 copy-done
  168.0 0.0 copy-done.6
  168.0 5.3 %convolution_convert_fusion = bf16[1024,128]{1,0:T(8,128)(2,1)} fusion(bf16[64,128]{1,0:T(8,128)(2,1)S(1)} %copy-done, bf16[16,208,1024]{2,1,0:T(8,128)(2,1)} %all-gather.9.cloned.1.call-done, bf16[16,64,208]{1,2,0:T(8,128)(2,1)S(1)} %bitcast.56, f32[64]{0:T(128)S(1)} %copy-done.6), kind=kOutput, calls=%fused_computation.6 | convolution fusion | flops 453312512 | bytes 7520512 | tf_op jit(solution)/shard_map/dot_general | solution.py:126
  173.3 4.6 %all-to-all-start = ((bf16[16,64,128]{2,1,0:T(8,128)(2,1)}), bf16[16,64,128]{2,1,0:T(8,128)(2,1)S(1)}, u32[]{:S(2)}, u32[]{:S(2)}) async-start(bf16[16,64,128]{2,1,0:T(8,128)(2,1)} %bitcast.16), calls=%async_computation | async-start | bytes 524288 | tf_op jit(solution)/shard_map/all_to_all | solution.py:27
  177.9 0.8 dynamic_slice.7
  178.6 8.9 %all-to-all-done = bf16[16,64,128]{2,1,0:T(8,128)(2,1)S(1)} async-done(((bf16[16,64,128]{2,1,0:T(8,128)(2,1)}), bf16[16,64,128]{2,1,0:T(8,128)(2,1)S(1)}, u32[]{:S(2)}, u32[]{:S(2)}) %all-to-all-start) | async-done | bytes 262176 | tf_op jit(solution)/shard_map/all_to_all | solution.py:27
  187.5 4.9 %all-gather.11.cloned.1.call-done = bf16[4096,128]{1,0:T(8,128)(2,1)} async-done(((bf16[1024,128]{1,0:T(8,128)(2,1)}), bf16[4096,128]{1,0:T(8,128)(2,1)}) %all-gather.11.cloned.1.call-update) | async-done | bytes 1048592 | tf_op jit(solution)/shard_map/all_gather | solution.py:15
  192.5 1.8 fusion.14
  194.3 0.5 exponential_reduce_fusion
  194.8 16.6 %all_to_all.11 = f32[16,1,64]{2,1,0:T(1,128)S(1)} all-to-all(f32[16,1,64]{2,1,0:T(1,128)S(1)} %broadcast_in_dim.15), channel_id=1, replica_groups=mesh['batch_0'=4,'batch_1'=4,'field'=2,'dim'=8] {'field','dim'}, dimensions={0} | all-to-all | bytes 8192 | tf_op jit(solution)/shard_map/all_to_all | solution.py:39
  211.4 0.5 broadcast.18
  211.9 0.7 reduce.7
  212.6 0.7 reshape.64
  (9 shorter events, 0.1 us)
Async XLA Ops:
  7.2 160.8 %copy-start = (bf16[64,128]{1,0:T(8,128)(2,1)S(1)}, bf16[64,128]{1,0:T(8,128)(2,1)}, u32[]{:S(2)}) copy-start(bf16[64,128]{1,0:T(8,128)(2,1)} %param.14) | copy-start | bytes 49156
  7.2 55.3 %all-gather.5.cloned.1.call-start = ((), (), s32[]{:S(2)}) async-start(), calls=%async_computation.2 | async-start | bytes 7241728 | tf_op jit(solution)/shard_map/all_gather | solution.py:64
  7.9 107.3 %all-gather.7.cloned.1.call-start = ((), (), s32[]{:S(2)}) async-start(), calls=%async_computation.3 | async-start | bytes 7241728 | tf_op jit(solution)/shard_map/all_gather | solution.py:64
  19.1 11.0 %copy-start.5 = (f32[2,13,16]{2,0,1:T(2,128)S(1)}, f32[2,13,16]{2,0,1:T(2,128)}, u32[]{:S(2)}) copy-start(f32[2,13,16]{2,0,1:T(2,128)} %param.11) | copy-start | bytes 4996
  62.5 4.6 %copy-start.1 = (bf16[13,16,1024]{2,1,0:T(8,128)(2,1)S(1)}, bf16[13,16,1024]{2,1,0:T(8,128)(2,1)}, u32[]{:S(2)}) copy-start(bf16[13,16,1024]{2,1,0:T(8,128)(2,1)} %param.9) | copy-start | bytes 1277956
  68.0 100.0 %all-gather.9.cloned.1.call-start = ((), (), s32[]{:S(2)}) async-start(), calls=%async_computation.4 | async-start | bytes 7241728 | tf_op jit(solution)/shard_map/all_gather | solution.py:123
  115.2 4.7 %copy-start.2 = (bf16[13,16,1024]{2,1,0:T(8,128)(2,1)S(1)}, bf16[13,16,1024]{2,1,0:T(8,128)(2,1)}, u32[]{:S(2)}) copy-start(bf16[13,16,1024]{2,1,0:T(8,128)(2,1)} %fusion.7) | copy-start | bytes 1277956
  115.2 5.7 %copy-start.4 = (bf16[256,128]{1,0:T(8,128)(2,1)S(1)}, bf16[256,128]{1,0:T(8,128)(2,1)}, u32[]{:S(2)}) copy-start(bf16[256,128]{1,0:T(8,128)(2,1)} %param.16) | copy-start | bytes 196612
  119.8 11.6 %copy-start.3 = (bf16[64,26,128]{2,0,1:T(8,128)(2,1)S(1)}, bf16[64,26,128]{2,0,1:T(8,128)(2,1)}, u32[]{:S(2)}) copy-start(bf16[64,26,128]{2,0,1:T(8,128)(2,1)} %param.12) | copy-start | bytes 1277956
  119.8 48.2 %copy-start.6 = (f32[64]{0:T(128)S(1)}, f32[64]{0:T(128)}, u32[]{:S(2)}) copy-start(f32[64]{0:T(128)} %param.13) | copy-start | bytes 772
  120.8 71.6 %all-gather.11.cloned.1.call-start = ((), (), s32[]{:S(2)}) async-start(), calls=%async_computation.5 | async-start | bytes 1310720 | tf_op jit(solution)/shard_map/all_gather | solution.py:15
  173.3 14.2 %all-to-all-start = ((bf16[16,64,128]{2,1,0:T(8,128)(2,1)}), bf16[16,64,128]{2,1,0:T(8,128)(2,1)S(1)}, u32[]{:S(2)}, u32[]{:S(2)}) async-start(bf16[16,64,128]{2,1,0:T(8,128)(2,1)} %bitcast.16), calls=%async_computation | async-start | bytes 524288 | tf_op jit(solution)/shard_map/all_to_all | solution.py:27
Sparse Core Ops, SparseCore 0:
  9.8 52.6 all-gather.4
  68.1 46.9 all-gather.6
  121.0 46.9 all-gather.8
  169.7 22.7 all-gather.10
where the time goes:
time: 220 us
  waiting for transfers between devices  110 us (50%)
  local copies, waits for them, and re-layouts  44.9 us (20%)
  blocking collectives  27 us (12%)
  matrix products  16.3 us (7%)
  between operations  13.9 us (6%)
  starting transfers between devices  4.74 us (2%)
  other arithmetic  3.03 us (1%)
    all_gather x2, waiting for transfers between devices, cross_flat(): lax.all_gather(flattened, ('field', 'dim'), axis=0, tiled=True)  59.2 us
    all_gather x1, waiting for transfers between devices, body(): lax.all_gather(flattened, ('field', 'dim'), axis=0, tiled=True)  36 us
    transpose x3, local copies, waits for them, and re-layouts, by_device(): shaped = shaped.transpose(1, 3, 0, 2, 4)  22.3 us
    another operation x2, local copies, waits for them, and re-layouts, by_device(): weights.reshape(out_count, field_count, fields_all // field_count, dim_co...  17.4 us
    all_to_all x1, blocking collectives, sent_to_all(): return lax.all_to_all(copies, axis, split_axis=0, concat_axis=0, tiled=True)  16.6 us
    all_gather x1, blocking collectives, whole_of(): nearer = lax.all_gather(x, axes[-1], axis=dim, tiled=True)  10.4 us
    dot_general x2, matrix products, row_adder(): jnp.einsum('kib,koi->ob', shards, blocks, preferred_element_type=jnp.floa...  9.24 us
    all_to_all x1, waiting for transfers between devices, summed_on_arrival(): pieces = lax.all_to_all(cut_along(x, dim, length), axis, 0, 0, tiled=True)  8.89 us
  transfers between devices with their start and end apart: 5, of which 5 were waited for; matrix products, arithmetic and copies ran while one was open for 22% of the time, Pallas kernels for 0%

commit v1 on v0

--- a/solution.py
+++ b/solution.py
@@ -7,6 +7,24 @@
 
 CROSS = 2
 BATCH = ("batch_0", "batch_1")
+
+
+def ring_gather(value, axis, dim):
+    ways, here, step = (lax.axis_size(axis), lax.axis_index(axis), value.shape[dim])
+    dims = [n * ways if d == dim else n for d, n in enumerate(value.shape)]
+    full = lax.dynamic_update_slice_in_dim(
+        jnp.zeros(dims, value.dtype), value, here * step, axis=dim
+    )
+    going_up = going_down = value
+    for far in range(1, ways // 2 + 1):
+        going_up = lax.ppermute(going_up, axis, [(d, (d + 1) % ways) for d in range(ways)])
+        full = lax.dynamic_update_slice_in_dim(full, going_up, (here - far) % ways * step, axis=dim)
+        if 2 * far < ways:
+            going_down = lax.ppermute(going_down, axis, [(d, (d - 1) % ways) for d in range(ways)])
+            full = lax.dynamic_update_slice_in_dim(
+                full, going_down, (here + far) % ways * step, axis=dim
+            )
+    return full
 
 
 def whole_of(x, axes, dim):
@@ -119,9 +137,7 @@
         current = next_layer(anchor, current, product, cross_bias[level_idx])
     tower_blocks = by_device(tower_weight, field_count, dim_count)
     flattened = current.reshape(1, column_count, row_count)
-    tower_pre = row_adder(
-        tower_blocks, lax.all_gather(flattened, ("field", "dim"), axis=0, tiled=True)
-    )
+    tower_pre = row_adder(tower_blocks, ring_gather(flattened, ("field", "dim"), 0))
     hidden = jax.nn.relu(tower_pre + tower_bias[:, None]).astype(jnp.bfloat16)
     partial_value = lax.dot_general(
         hidden, query_weight, (((0,), (0,)), ((), ())), preferred_element_type=jnp.float32

time: 220 us -> 275 us (1.25)
  starting transfers between devices: 4.74 us -> 29.2 us
  local copies, waits for them, and re-layouts: 44.9 us -> 66.4 us
  waiting for transfers between devices: 110 us -> 120 us
  blocking collectives: 27 us -> 23.3 us
    ppermute x0 -> x15, waiting for transfers between devices: none -> 52 us  [the longest x8 44.4 us: ring_gather(): lax.ppermute(going_up, axis, [(d, (d + 1) % ways) for d in range(ways)])]
    all_gather x1 -> x0, waiting for transfers between devices: 36 us -> none  [body(): lax.all_gather(flattened, ('field', 'dim'), axis=0, tiled=True)]
    ppermute x0 -> x15, starting transfers between devices: none -> 25.6 us  [the longest x7 23.9 us: ring_gather(): lax.ppermute(going_down, axis, [(d, (d - 1) % ways) for d in range(ways)])]
    dynamic_update_slice x0 -> x16, local copies, waits for them, and re-layouts: none -> 16.7 us  [the longest x8 8.37 us: ring_gather(): lax.dynamic_update_slice_in_dim(full, going_up, (here - far) % ways * ste...]
    all_gather x1, waiting for transfers between devices: 4.93 us -> 0.03 us  [whole_of(): nearer = lax.all_gather(x, axes[-1], axis=dim, tiled=True)]
    all_to_all x1, blocking collectives: 16.6 us -> 12 us  [sent_to_all(): return lax.all_to_all(copies, axis, split_axis=0, concat_axis=0, tiled=True)]
    broadcast_in_dim x0 -> x1, local copies, waits for them, and re-layouts: none -> 3.71 us  [ring_gather(): jnp.zeros(dims, value.dtype)]
  transfers between devices with their start and end apart: 5 -> 19, of which waited for: 5 -> 12; matrix products, arithmetic and copies ran while one was open for 22% -> 26% of each run, Pallas kernels for 0% -> 0%
where the time goes in v1:
time: 275 us; the launch traced here: 274 us
  waiting for transfers between devices  120 us (44%)
  local copies, waits for them, and re-layouts  66.4 us (24%)
  starting transfers between devices  29.2 us (11%)
  blocking collectives  23.3 us (8%)
  matrix products  16.4 us (6%)
  between operations  16.1 us (6%)
    all_gather x2, waiting for transfers between devices, cross_flat(): lax.all_gather(flattened, ('field', 'dim'), axis=0, tiled=True)  59.2 us
    ppermute x8, waiting for transfers between devices, ring_gather(): lax.ppermute(going_up, axis, [(d, (d + 1) % ways) for d in range(ways)])  44.4 us
    ppermute x7, starting transfers between devices, ring_gather(): lax.ppermute(going_down, axis, [(d, (d - 1) % ways) for d in range(ways)])  23.9 us
    transpose x3, local copies, waits for them, and re-layouts, by_device(): shaped = shaped.transpose(1, 3, 0, 2, 4)  22.2 us
    another operation x2, local copies, waits for them, and re-layouts, by_device(): weights.reshape(out_count, field_count, fields_all // field_count, dim_co...  17.4 us
    all_to_all x1, blocking collectives, sent_to_all(): return lax.all_to_all(copies, axis, split_axis=0, concat_axis=0, tiled=True)  12 us
    all_gather x1, blocking collectives, whole_of(): nearer = lax.all_gather(x, axes[-1], axis=dim, tiled=True)  11.3 us
    dot_general x2, matrix products, row_adder(): jnp.einsum('kib,koi->ob', shards, blocks, preferred_element_type=jnp.floa...  9.27 us
  transfers between devices with their start and end apart: 19, of which 12 were waited for; matrix products, arithmetic and copies ran while one was open for 26% of the time, Pallas kernels for 0%

profile of v1, /device:TPU:1, one launch (start us, length us, event | category | flops | bytes accessed | tf_op | source)
XLA Modules:
  0.0 273.7 jit_solution(653335440521482988)
XLA Ops:
  8.8 2.2 fusion.13
  11.3 8.7 %reshape_squeeze.8 = bf16[208,2,13,8,16]{4,3,0,2,1:T(8,128)(2,1)} reshape(bf16[1,13,16,26,128]{4,2,1,3,0:T(8,128)(2,1)S(1)} %copy.19) | data formatting | bytes 2768896 | tf_op jit(solution)/shard_map/reshape;squeeze | solution.py:66
  20.0 10.9 %copy.20 = bf16[2,8,208,13,16]{2,4,3,1,0:T(8,128)(2,1)S(1)} copy(bf16[2,8,208,13,16]{4,1,2,3,0:T(8,128)(2,1)} %bitcast.52) | data formatting | bytes 2768896 | tf_op jit(solution)/shard_map/transpose | solution.py:69
  31.1 32.3 %all-gather.4.cloned.1.call-done = bf16[16,208,1024]{2,1,0:T(8,128)(2,1)} async-done(((bf16[1,208,1024]{2,1,0:T(8,128)(2,1)}), bf16[16,208,1024]{2,1,0:T(8,128)(2,1)}) %all-gather.4.cloned.1.call-update) | async-done | bytes 6815760 | tf_op jit(solution)/shard_map/all_gather | solution.py:82
  63.3 4.6 %fusion = f32[208,1024]{1,0:T(8,128)S(1)} fusion(bf16[16,208,208]{1,2,0:T(8,128)(2,1)S(1)} %bitcast.54, bf16[16,208,1024]{2,1,0:T(8,128)(2,1)} %all-gather.4.cloned.1.call-done, f32[208]{0:T(256)S(1)} %add.175), kind=kOutput, calls=%fused_computation.4 | convolution fusion | flops 1417887744 | bytes 9052992 | tf_op jit(solution)/shard_map/kib,koi->ob/dot_general | solution.py:76
  68.0 0.9 fusion.7
  69.2 8.7 %reshape_squeeze.9 = bf16[208,2,13,8,16]{4,3,0,2,1:T(8,128)(2,1)} reshape(bf16[1,13,16,26,128]{4,2,1,3,0:T(8,128)(2,1)S(1)} %copy.22) | data formatting | bytes 2768896 | tf_op jit(solution)/shard_map/reshape;squeeze | solution.py:66
  77.9 11.2 %copy.23 = bf16[2,8,208,13,16]{2,4,3,1,0:T(8,128)(2,1)S(1)} copy(bf16[2,8,208,13,16]{4,1,2,3,0:T(8,128)(2,1)} %bitcast.53) | data formatting | bytes 2768896 | tf_op jit(solution)/shard_map/transpose | solution.py:69
  89.1 26.9 %all-gather.6.cloned.1.call-done = bf16[16,208,1024]{2,1,0:T(8,128)(2,1)} async-done(((bf16[1,208,1024]{2,1,0:T(8,128)(2,1)}), bf16[16,208,1024]{2,1,0:T(8,128)(2,1)}) %all-gather.6.cloned.1.call-update) | async-done | bytes 6815760 | tf_op jit(solution)/shard_map/all_gather | solution.py:82
  116.0 4.6 %fusion.1 = f32[1024,208]{0,1:T(8,128)S(1)} fusion(bf16[16,208,1024]{2,1,0:T(8,128)(2,1)} %all-gather.6.cloned.1.call-done, bf16[16,208,208]{1,2,0:T(8,128)(2,1)S(1)} %bitcast.60, f32[208]{0:T(256)S(1)} %add.179), kind=kOutput, calls=%fused_computation.5 | convolution fusion | flops 1417887744 | bytes 9052992 | tf_op jit(solution)/shard_map/kib,koi->ob/dot_general | solution.py:76
  121.2 2.7 collective-permute-start.1
  123.9 10.0 %collective-permute-done = bf16[1,208,1024]{2,1,0:T(8,128)(2,1)S(1)} collective-permute-done((bf16[1,208,1024]{2,1,0:T(8,128)(2,1)S(1)}, bf16[1,208,1024]{2,1,0:T(8,128)(2,1)S(1)}, u32[]{:S(2)}, u32[]{:S(2)}) %collective-permute-start) | collective-permute-done | bytes 426016 | tf_op jit(solution)/shard_map/ppermute | solution.py:20
  133.9 2.9 %collective-permute-start.3 = (bf16[1,208,1024]{2,1,0:T(8,128)(2,1)S(1)}, bf16[1,208,1024]{2,1,0:T(8,128)(2,1)S(1)}, u32[]{:S(2)}, u32[]{:S(2)}) collective-permute-start(bf16[1,208,1024]{2,1,0:T(8,128)(2,1)S(1)} %collective-permute-done.1), channel_id=1, source_target_pairs={{0,15},{1,0},{2,1},{3,2},{4,3},{5,4},{6,5},{7,6},{8,7},{9,8},{10,9... | collective-permute-start | bytes 1277960 | tf_op jit(solution)/shard_map/ppermute | solution.py:23
  136.9 9.9 %collective-permute-done.2 = bf16[1,208,1024]{2,1,0:T(8,128)(2,1)S(1)} collective-permute-done((bf16[1,208,1024]{2,1,0:T(8,128)(2,1)S(1)}, bf16[1,208,1024]{2,1,0:T(8,128)(2,1)S(1)}, u32[]{:S(2)}, u32[]{:S(2)}) %collective-permute-start.2) | collective-permute-done | bytes 426016 | tf_op jit(solution)/shard_map/ppermute | solution.py:20
  146.8 3.0 %collective-permute-start.5 = (bf16[1,208,1024]{2,1,0:T(8,128)(2,1)S(1)}, bf16[1,208,1024]{2,1,0:T(8,128)(2,1)}, u32[]{:S(2)}, u32[]{:S(2)}) collective-permute-start(bf16[1,208,1024]{2,1,0:T(8,128)(2,1)S(1)} %collective-permute-done.3), channel_id=1, source_target_pairs={{0,15},{1,0},{2,1},{3,2},{4,3},{5,4},{6,5},{7,6},{8,7},{9,8},{10,9... | collective-permute-start | bytes 1277960 | tf_op jit(solution)/shard_map/ppermute | solution.py:23
  149.8 9.9 %collective-permute-done.4 = bf16[1,208,1024]{2,1,0:T(8,128)(2,1)S(1)} collective-permute-done((bf16[1,208,1024]{2,1,0:T(8,128)(2,1)S(1)}, bf16[1,208,1024]{2,1,0:T(8,128)(2,1)S(1)}, u32[]{:S(2)}, u32[]{:S(2)}) %collective-permute-start.4) | collective-permute-done | bytes 426016 | tf_op jit(solution)/shard_map/ppermute | solution.py:20
  159.7 3.0 %collective-permute-start.7 = (bf16[1,208,1024]{2,1,0:T(8,128)(2,1)}, bf16[1,208,1024]{2,1,0:T(8,128)(2,1)S(1)}, u32[]{:S(2)}, u32[]{:S(2)}) collective-permute-start(bf16[1,208,1024]{2,1,0:T(8,128)(2,1)} %collective-permute-done.5), channel_id=1, source_target_pairs={{0,15},{1,0},{2,1},{3,2},{4,3},{5,4},{6,5},{7,6},{8,7},{9,8},{10,9... | collective-permute-start | bytes 1277960 | tf_op jit(solution)/shard_map/ppermute | solution.py:23
  162.8 9.9 %collective-permute-done.6 = bf16[1,208,1024]{2,1,0:T(8,128)(2,1)S(1)} collective-permute-done((bf16[1,208,1024]{2,1,0:T(8,128)(2,1)S(1)}, bf16[1,208,1024]{2,1,0:T(8,128)(2,1)S(1)}, u32[]{:S(2)}, u32[]{:S(2)}) %collective-permute-start.6) | collective-permute-done | bytes 426016 | tf_op jit(solution)/shard_map/ppermute | solution.py:20
  172.7 11.3 %all_gather.14 = bf16[1024,128]{1,0:T(8,128)(2,1)} all-gather(bf16[256,128]{1,0:T(8,128)(2,1)S(1)} %copy-done.10), channel_id=1, replica_groups=mesh['batch_0'=4,'batch_1'=4,'field'=2,'dim'=8] {'batch_1'}, dimensions={0}, use_global_device_ids=true | all-gather | bytes 327680 | tf_op jit(solution)/shard_map/all_gather | solution.py:33
  184.2 1.4 copy.25
  185.9 3.7 %broadcast_in_dim.16 = bf16[16,208,1024]{2,1,0:T(8,128)(2,1)} broadcast(bf16[]{:T(256)} %constant.98.clone.1), dimensions={} | broadcast | bytes 6815746 | tf_op jit(solution)/shard_map/broadcast_in_dim | solution.py:16
  189.7 0.8 constant_dynamic-update-slice_fusion.15
  190.5 0.8 constant_dynamic-update-slice_fusion.14
  191.3 4.9 %collective-permute-start.9 = (bf16[1,208,1024]{2,1,0:T(8,128)(2,1)S(1)}, bf16[1,208,1024]{2,1,0:T(8,128)(2,1)S(1)}, u32[]{:S(2)}, u32[]{:S(2)}) collective-permute-start(bf16[1,208,1024]{2,1,0:T(8,128)(2,1)S(1)} %collective-permute-done.7), channel_id=1, source_target_pairs={{0,15},{1,0},{2,1},{3,2},{4,3},{5,4},{6,5},{7,6},{8,7},{9,8},{10,9... | collective-permute-start | bytes 1277960 | tf_op jit(solution)/shard_map/ppermute | solution.py:23
  197.0 0.8 constant_dynamic-update-slice_fusion.12
  197.8 1.8 constant_dynamic-update-slice_fusion.11
  199.6 1.8 constant_dynamic-update-slice_fusion.10
  201.4 2.0 collective-permute-done.9
  203.4 3.7 %collective-permute-start.11 = (bf16[1,208,1024]{2,1,0:T(8,128)(2,1)S(1)}, bf16[1,208,1024]{2,1,0:T(8,128)(2,1)S(1)}, u32[]{:S(2)}, u32[]{:S(2)}) collective-permute-start(bf16[1,208,1024]{2,1,0:T(8,128)(2,1)S(1)} %collective-permute-done.9), channel_id=1, source_target_pairs={{0,15},{1,0},{2,1},{3,2},{4,3},{5,4},{6,5},{7,6},{8,7},{9,8},{10,9... | collective-permute-start | bytes 1277960 | tf_op jit(solution)/shard_map/ppermute | solution.py:23
  207.1 1.8 constant_dynamic-update-slice_fusion.9
  208.9 0.8 constant_dynamic-update-slice_fusion.8
  209.7 0.8 constant_dynamic-update-slice_fusion.7
  210.5 1.8 constant_dynamic-update-slice_fusion.6
  212.3 2.3 collective-permute-done.11
  214.7 3.7 %collective-permute-start.13 = (bf16[1,208,1024]{2,1,0:T(8,128)(2,1)S(1)}, bf16[1,208,1024]{2,1,0:T(8,128)(2,1)S(1)}, u32[]{:S(2)}, u32[]{:S(2)}) collective-permute-start(bf16[1,208,1024]{2,1,0:T(8,128)(2,1)S(1)} %collective-permute-done.11), channel_id=1, source_target_pairs={{0,15},{1,0},{2,1},{3,2},{4,3},{5,4},{6,5},{7,6},{8,7},{9,8},{10,9... | collective-permute-start | bytes 1277960 | tf_op jit(solution)/shard_map/ppermute | solution.py:23
  218.3 0.8 constant_dynamic-update-slice_fusion.5
  219.3 1.3 collective-permute-start.14
  220.6 0.8 constant_dynamic-update-slice_fusion.4
  221.4 0.8 constant_dynamic-update-slice_fusion.3
  223.0 3.2 %collective-permute-done.13 = bf16[1,208,1024]{2,1,0:T(8,128)(2,1)S(1)} collective-permute-done((bf16[1,208,1024]{2,1,0:T(8,128)(2,1)S(1)}, bf16[1,208,1024]{2,1,0:T(8,128)(2,1)S(1)}, u32[]{:S(2)}, u32[]{:S(2)}) %collective-permute-start.13) | collective-permute-done | bytes 426016 | tf_op jit(solution)/shard_map/ppermute | solution.py:23
  226.2 0.8 constant_dynamic-update-slice_fusion.1
  227.0 4.5 %collective-permute-done.14 = bf16[1,208,1024]{2,1,0:T(8,128)(2,1)S(1)} collective-permute-done((bf16[1,208,1024]{2,1,0:T(8,128)(2,1)S(1)}, bf16[1,208,1024]{2,1,0:T(8,128)(2,1)S(1)}, u32[]{:S(2)}, u32[]{:S(2)}) %collective-permute-start.14) | collective-permute-done | bytes 426016 | tf_op jit(solution)/shard_map/ppermute | solution.py:20
  231.5 0.8 constant_dynamic-update-slice_fusion
  232.3 5.3 %convolution_convert_fusion = bf16[1024,128]{1,0:T(8,128)(2,1)} fusion(bf16[64,128]{1,0:T(8,128)(2,1)S(1)} %copy-done, bf16[16,208,1024]{2,1,0:T(8,128)(2,1)} %constant_dynamic-update-slice_fusion, bf16[16,64,208]{1,2,0:T(8,128)(2,1)S(1)} %bitcast.58, f32[64]{0:T(128)S(1)} %copy-done.12), kind=kOutput, calls=%fused_computation.6 | convolution fusion | flops 453312512 | bytes 7520512 | tf_op jit(solution)/shard_map/dot_general | solution.py:142
  237.6 3.4 %all-to-all-start = ((bf16[16,64,128]{2,1,0:T(8,128)(2,1)}), bf16[16,64,128]{2,1,0:T(8,128)(2,1)S(1)}, u32[]{:S(2)}, u32[]{:S(2)}) async-start(bf16[16,64,128]{2,1,0:T(8,128)(2,1)} %bitcast.16), calls=%async_computation | async-start | bytes 524288 | tf_op jit(solution)/shard_map/all_to_all | solution.py:45
  241.8 8.2 %all-to-all-done = bf16[16,64,128]{2,1,0:T(8,128)(2,1)S(1)} async-done(((bf16[16,64,128]{2,1,0:T(8,128)(2,1)}), bf16[16,64,128]{2,1,0:T(8,128)(2,1)S(1)}, u32[]{:S(2)}, u32[]{:S(2)}) %all-to-all-start) | async-done | bytes 262176 | tf_op jit(solution)/shard_map/all_to_all | solution.py:45
  250.1 1.8 fusion.14
  252.4 12.0 %all_to_all.11 = f32[16,1,64]{2,1,0:T(1,128)S(1)} all-to-all(f32[16,1,64]{2,1,0:T(1,128)S(1)} %broadcast_in_dim.19), channel_id=1, replica_groups=mesh['batch_0'=4,'batch_1'=4,'field'=2,'dim'=8] {'field','dim'}, dimensions={0} | all-to-all | bytes 8192 | tf_op jit(solution)/shard_map/all_to_all | solution.py:57
  (65 shorter events, 7.1 us)
Async XLA Ops:
  8.0 224.3 %copy-start = (bf16[64,128]{1,0:T(8,128)(2,1)S(1)}, bf16[64,128]{1,0:T(8,128)(2,1)}, u32[]{:S(2)}) copy-start(bf16[64,128]{1,0:T(8,128)(2,1)} %param.14) | copy-start | bytes 49156
  8.0 55.3 %all-gather.4.cloned.1.call-start = ((), (), s32[]{:S(2)}) async-start(), calls=%async_computation.2 | async-start | bytes 7241728 | tf_op jit(solution)/shard_map/all_gather | solution.py:82
  8.7 107.3 %all-gather.6.cloned.1.call-start = ((), (), s32[]{:S(2)}) async-start(), calls=%async_computation.3 | async-start | bytes 7241728 | tf_op jit(solution)/shard_map/all_gather | solution.py:82
  20.0 11.0 %copy-start.11 = (f32[2,13,16]{2,0,1:T(2,128)S(1)}, f32[2,13,16]{2,0,1:T(2,128)}, u32[]{:S(2)}) copy-start(f32[2,13,16]{2,0,1:T(2,128)} %param.11) | copy-start | bytes 4996
  63.3 4.6 %copy-start.1 = (bf16[13,16,1024]{2,1,0:T(8,128)(2,1)S(1)}, bf16[13,16,1024]{2,1,0:T(8,128)(2,1)}, u32[]{:S(2)}) copy-start(bf16[13,16,1024]{2,1,0:T(8,128)(2,1)} %param.9) | copy-start | bytes 1277956
  68.9 181.2 %all-gather.8.cloned.1.call-start = ((), (), s32[]{:S(2)}) async-start(), calls=%async_computation.4 | async-start | bytes 1310720 | tf_op jit(solution)/shard_map/all_gather | solution.py:33
  89.0 31.7 %copy-start.2 = (bf16[13,16,1024]{2,1,0:T(8,128)(2,1)S(1)}, bf16[13,16,1024]{2,1,0:T(8,128)(2,1)}, u32[]{:S(2)}) copy-start(bf16[13,16,1024]{2,1,0:T(8,128)(2,1)} %fusion.7) | copy-start | bytes 1277956
  116.0 56.6 %copy-start.10 = (bf16[256,128]{1,0:T(8,128)(2,1)S(1)}, bf16[256,128]{1,0:T(8,128)(2,1)}, u32[]{:S(2)}) copy-start(bf16[256,128]{1,0:T(8,128)(2,1)} %param.16) | copy-start | bytes 196612
  120.9 76.9 %copy-start.3 = (bf16[13,16,1024]{2,1,0:T(8,128)(2,1)}, bf16[13,16,1024]{2,1,0:T(8,128)(2,1)S(1)}, u32[]{:S(2)}) copy-start(bf16[13,16,1024]{2,1,0:T(8,128)(2,1)S(1)} %fusion.6) | copy-start | bytes 1277956
  120.9 13.0 %collective-permute-start = (bf16[1,208,1024]{2,1,0:T(8,128)(2,1)S(1)}, bf16[1,208,1024]{2,1,0:T(8,128)(2,1)S(1)}, u32[]{:S(2)}, u32[]{:S(2)}) collective-permute-start(bf16[1,208,1024]{2,1,0:T(8,128)(2,1)S(1)} %bitcast.61), channel_id=1, source_target_pairs={{0,1},{1,2},{2,3},{3,4},{4,5},{5,6},{6,7},{7,8},{8,9},{9,10},{10,1... | collective-permute-start | bytes 1277960 | tf_op jit(solution)/shard_map/ppermute | solution.py:20
  121.2 12.7 %collective-permute-start.1 = (bf16[1,208,1024]{2,1,0:T(8,128)(2,1)S(1)}, bf16[1,208,1024]{2,1,0:T(8,128)(2,1)S(1)}, u32[]{:S(2)}, u32[]{:S(2)}) collective-permute-start(bf16[1,208,1024]{2,1,0:T(8,128)(2,1)S(1)} %bitcast.62), channel_id=1, source_target_pairs={{0,15},{1,0},{2,1},{3,2},{4,3},{5,4},{6,5},{7,6},{8,7},{9,8},{10,9... | collective-permute-start | bytes 1277960 | tf_op jit(solution)/shard_map/ppermute | solution.py:23
  133.9 3.0 %copy-start.8 = (bf16[1,208,1024]{2,1,0:T(8,128)(2,1)}, bf16[1,208,1024]{2,1,0:T(8,128)(2,1)S(1)}, u32[]{:S(2)}) copy-start(bf16[1,208,1024]{2,1,0:T(8,128)(2,1)S(1)} %collective-permute-done) | copy-start | bytes 1277956
  133.9 12.9 %collective-permute-start.2 = (bf16[1,208,1024]{2,1,0:T(8,128)(2,1)S(1)}, bf16[1,208,1024]{2,1,0:T(8,128)(2,1)S(1)}, u32[]{:S(2)}, u32[]{:S(2)}) collective-permute-start(bf16[1,208,1024]{2,1,0:T(8,128)(2,1)S(1)} %collective-permute-done), channel_id=1, source_target_pairs={{0,1},{1,2},{2,3},{3,4},{4,5},{5,6},{6,7},{7,8},{8,9},{9,10},{10,1... | collective-permute-start | bytes 1277960 | tf_op jit(solution)/shard_map/ppermute | solution.py:20
  133.9 15.9 %copy-start.5 = (bf16[1,208,1024]{2,1,0:T(8,128)(2,1)}, bf16[1,208,1024]{2,1,0:T(8,128)(2,1)S(1)}, u32[]{:S(2)}) copy-start(bf16[1,208,1024]{2,1,0:T(8,128)(2,1)S(1)} %collective-permute-done.1) | copy-start | bytes 1277956
  133.9 12.9 %collective-permute-start.3 = (bf16[1,208,1024]{2,1,0:T(8,128)(2,1)S(1)}, bf16[1,208,1024]{2,1,0:T(8,128)(2,1)S(1)}, u32[]{:S(2)}, u32[]{:S(2)}) collective-permute-start(bf16[1,208,1024]{2,1,0:T(8,128)(2,1)S(1)} %collective-permute-done.1), channel_id=1, source_target_pairs={{0,15},{1,0},{2,1},{3,2},{4,3},{5,4},{6,5},{7,6},{8,7},{9,8},{10,9... | collective-permute-start | bytes 1277960 | tf_op jit(solution)/shard_map/ppermute | solution.py:23
  146.8 12.9 %collective-permute-start.4 = (bf16[1,208,1024]{2,1,0:T(8,128)(2,1)S(1)}, bf16[1,208,1024]{2,1,0:T(8,128)(2,1)S(1)}, u32[]{:S(2)}, u32[]{:S(2)}) collective-permute-start(bf16[1,208,1024]{2,1,0:T(8,128)(2,1)S(1)} %collective-permute-done.2), channel_id=1, source_target_pairs={{0,1},{1,2},{2,3},{3,4},{4,5},{5,6},{6,7},{7,8},{8,9},{9,10},{10,1... | collective-permute-start | bytes 1277960 | tf_op jit(solution)/shard_map/ppermute | solution.py:20
  146.8 25.8 %copy-start.4 = (bf16[1,208,1024]{2,1,0:T(8,128)(2,1)}, bf16[1,208,1024]{2,1,0:T(8,128)(2,1)S(1)}, u32[]{:S(2)}) copy-start(bf16[1,208,1024]{2,1,0:T(8,128)(2,1)S(1)} %collective-permute-done.3) | copy-start | bytes 1277956
  146.8 12.9 %collective-permute-start.5 = (bf16[1,208,1024]{2,1,0:T(8,128)(2,1)S(1)}, bf16[1,208,1024]{2,1,0:T(8,128)(2,1)}, u32[]{:S(2)}, u32[]{:S(2)}) collective-permute-start(bf16[1,208,1024]{2,1,0:T(8,128)(2,1)S(1)} %collective-permute-done.3), channel_id=1, source_target_pairs={{0,15},{1,0},{2,1},{3,2},{4,3},{5,4},{6,5},{7,6},{8,7},{9,8},{10,9... | collective-permute-start | bytes 1277960 | tf_op jit(solution)/shard_map/ppermute | solution.py:23
  159.7 12.9 %copy-start.7 = (bf16[1,208,1024]{2,1,0:T(8,128)(2,1)}, bf16[1,208,1024]{2,1,0:T(8,128)(2,1)S(1)}, u32[]{:S(2)}) copy-start(bf16[1,208,1024]{2,1,0:T(8,128)(2,1)S(1)} %collective-permute-done.4) | copy-start | bytes 1277956
  159.7 12.9 %collective-permute-start.6 = (bf16[1,208,1024]{2,1,0:T(8,128)(2,1)S(1)}, bf16[1,208,1024]{2,1,0:T(8,128)(2,1)S(1)}, u32[]{:S(2)}, u32[]{:S(2)}) collective-permute-start(bf16[1,208,1024]{2,1,0:T(8,128)(2,1)S(1)} %collective-permute-done.4), channel_id=1, source_target_pairs={{0,1},{1,2},{2,3},{3,4},{4,5},{5,6},{6,7},{7,8},{8,9},{9,10},{10,1... | collective-permute-start | bytes 1277960 | tf_op jit(solution)/shard_map/ppermute | solution.py:20
  159.7 31.5 %collective-permute-start.7 = (bf16[1,208,1024]{2,1,0:T(8,128)(2,1)}, bf16[1,208,1024]{2,1,0:T(8,128)(2,1)S(1)}, u32[]{:S(2)}, u32[]{:S(2)}) collective-permute-start(bf16[1,208,1024]{2,1,0:T(8,128)(2,1)} %collective-permute-done.5), channel_id=1, source_target_pairs={{0,15},{1,0},{2,1},{3,2},{4,3},{5,4},{6,5},{7,6},{8,7},{9,8},{10,9... | collective-permute-start | bytes 1277960 | tf_op jit(solution)/shard_map/ppermute | solution.py:23
  172.6 24.3 %collective-permute-start.8 = (bf16[1,208,1024]{2,1,0:T(8,128)(2,1)S(1)}, bf16[1,208,1024]{2,1,0:T(8,128)(2,1)}, u32[]{:S(2)}, u32[]{:S(2)}) collective-permute-start(bf16[1,208,1024]{2,1,0:T(8,128)(2,1)S(1)} %collective-permute-done.6), channel_id=1, source_target_pairs={{0,1},{1,2},{2,3},{3,4},{4,5},{5,6},{6,7},{7,8},{8,9},{9,10},{10,1... | collective-permute-start | bytes 1277960 | tf_op jit(solution)/shard_map/ppermute | solution.py:20
  185.8 4.6 %copy-start.9 = (bf16[1,208,1024]{2,1,0:T(8,128)(2,1)S(1)}, bf16[1,208,1024]{2,1,0:T(8,128)(2,1)}, u32[]{:S(2)}) copy-start(bf16[1,208,1024]{2,1,0:T(8,128)(2,1)} %copy-done.8) | copy-start | bytes 1277956
  185.8 10.4 %copy-start.6 = (bf16[1,208,1024]{2,1,0:T(8,128)(2,1)S(1)}, bf16[1,208,1024]{2,1,0:T(8,128)(2,1)}, u32[]{:S(2)}) copy-start(bf16[1,208,1024]{2,1,0:T(8,128)(2,1)} %copy-done.5) | copy-start | bytes 1277956
  189.6 42.7 %copy-start.12 = (f32[64]{0:T(128)S(1)}, f32[64]{0:T(128)}, u32[]{:S(2)}) copy-start(f32[64]{0:T(128)} %param.13) | copy-start | bytes 772
  191.3 12.1 %collective-permute-start.9 = (bf16[1,208,1024]{2,1,0:T(8,128)(2,1)S(1)}, bf16[1,208,1024]{2,1,0:T(8,128)(2,1)S(1)}, u32[]{:S(2)}, u32[]{:S(2)}) collective-permute-start(bf16[1,208,1024]{2,1,0:T(8,128)(2,1)S(1)} %collective-permute-done.7), channel_id=1, source_target_pairs={{0,15},{1,0},{2,1},{3,2},{4,3},{5,4},{6,5},{7,6},{8,7},{9,8},{10,9... | collective-permute-start | bytes 1277960 | tf_op jit(solution)/shard_map/ppermute | solution.py:23
  197.0 11.9 %collective-permute-start.10 = (bf16[1,208,1024]{2,1,0:T(8,128)(2,1)}, bf16[1,208,1024]{2,1,0:T(8,128)(2,1)S(1)}, u32[]{:S(2)}, u32[]{:S(2)}) collective-permute-start(bf16[1,208,1024]{2,1,0:T(8,128)(2,1)} %collective-permute-done.8), channel_id=1, source_target_pairs={{0,1},{1,2},{2,3},{3,4},{4,5},{5,6},{6,7},{7,8},{8,9},{9,10},{10,1... | collective-permute-start | bytes 1277960 | tf_op jit(solution)/shard_map/ppermute | solution.py:20
  203.4 11.3 %collective-permute-start.11 = (bf16[1,208,1024]{2,1,0:T(8,128)(2,1)S(1)}, bf16[1,208,1024]{2,1,0:T(8,128)(2,1)S(1)}, u32[]{:S(2)}, u32[]{:S(2)}) collective-permute-start(bf16[1,208,1024]{2,1,0:T(8,128)(2,1)S(1)} %collective-permute-done.9), channel_id=1, source_target_pairs={{0,15},{1,0},{2,1},{3,2},{4,3},{5,4},{6,5},{7,6},{8,7},{9,8},{10,9... | collective-permute-start | bytes 1277960 | tf_op jit(solution)/shard_map/ppermute | solution.py:23
  208.9 10.4 %collective-permute-start.12 = (bf16[1,208,1024]{2,1,0:T(8,128)(2,1)S(1)}, bf16[1,208,1024]{2,1,0:T(8,128)(2,1)S(1)}, u32[]{:S(2)}, u32[]{:S(2)}) collective-permute-start(bf16[1,208,1024]{2,1,0:T(8,128)(2,1)S(1)} %collective-permute-done.10), channel_id=1, source_target_pairs={{0,1},{1,2},{2,3},{3,4},{4,5},{5,6},{6,7},{7,8},{8,9},{9,10},{10,1... | collective-permute-start | bytes 1277960 | tf_op jit(solution)/shard_map/ppermute | solution.py:20
  214.7 11.6 %collective-permute-start.13 = (bf16[1,208,1024]{2,1,0:T(8,128)(2,1)S(1)}, bf16[1,208,1024]{2,1,0:T(8,128)(2,1)S(1)}, u32[]{:S(2)}, u32[]{:S(2)}) collective-permute-start(bf16[1,208,1024]{2,1,0:T(8,128)(2,1)S(1)} %collective-permute-done.11), channel_id=1, source_target_pairs={{0,15},{1,0},{2,1},{3,2},{4,3},{5,4},{6,5},{7,6},{8,7},{9,8},{10,9... | collective-permute-start | bytes 1277960 | tf_op jit(solution)/shard_map/ppermute | solution.py:23
  219.3 12.3 %collective-permute-start.14 = (bf16[1,208,1024]{2,1,0:T(8,128)(2,1)S(1)}, bf16[1,208,1024]{2,1,0:T(8,128)(2,1)S(1)}, u32[]{:S(2)}, u32[]{:S(2)}) collective-permute-start(bf16[1,208,1024]{2,1,0:T(8,128)(2,1)S(1)} %collective-permute-done.12), channel_id=1, source_target_pairs={{0,1},{1,2},{2,3},{3,4},{4,5},{5,6},{6,7},{7,8},{8,9},{9,10},{10,1... | collective-permute-start | bytes 1277960 | tf_op jit(solution)/shard_map/ppermute | solution.py:20
  237.6 12.4 %all-to-all-start = ((bf16[16,64,128]{2,1,0:T(8,128)(2,1)}), bf16[16,64,128]{2,1,0:T(8,128)(2,1)S(1)}, u32[]{:S(2)}, u32[]{:S(2)}) async-start(bf16[16,64,128]{2,1,0:T(8,128)(2,1)} %bitcast.16), calls=%async_computation | async-start | bytes 524288 | tf_op jit(solution)/shard_map/all_to_all | solution.py:45
Sparse Core Ops, SparseCore 0:
  10.6 52.6 all-gather.3
  69.0 46.9 all-gather.5
Sparse Core Ops, SparseCore 1:
  184.1 24.1 all-gather.7
